TPU v7x, 32 devices: a whole 2x2x4 slice. The times are simulated.
32 devices in a mesh: node: 8 (over z, x), local: 4 (over y, core).
Axes of the slice: x: 2, y: 2, z: 4, core: 2. Of those that a mesh axis runs over, the one named last changes fastest.
Arguments:
- gate_pre: bfloat16 [3584, 15360], P('node', 'local'), may hold values from -6 to 6
- up_pre: bfloat16 [3584, 15360], P('node', 'local'), may hold values from -6 to 6
- out_grad: bfloat16 [3584, 4096], P('node', 'local'), may hold values from -6 to 6
Outputs:
- weight_grad: float32 [15360, 4096], P('local', 'node')
All inputs are finite; a program needn't handle non-finite values.
Results may differ from a plain program's by a relative error of at most 0.015.
Values may be sent and summed in bfloat16 or wider, within the bound.
A program may use at most 128 MiB of HBM per device.

v0:
```python
import functools

import jax
import jax.numpy as jnp
from jax import lax
from jax.experimental import pallas as pl
from jax.experimental.pallas import tpu as pltpu
from jax.sharding import PartitionSpec as P

WEIGHTS = (1,) * 15
TILE = 128


def chunks(units):
    tiles, total = units // TILE, sum(WEIGHTS)
    ends = [tiles * sum(WEIGHTS[: k + 1]) // total * TILE for k in range(len(WEIGHTS))]
    return list(zip([0] + ends[:-1], ends))


def kernel(
    n_node, n_local, hidden_ref, grad_ref, out_ref,
    whole, grads, going, coming,
    z_sem, x_sem, p_sem, g_sem, swap_sem, own_sem,
):
    wide = n_node // n_local
    halves = n_local // 2
    node, local = lax.axis_index("node"), lax.axis_index("local")
    z, x, y, c = node // wide, node % wide, local // 2, local % 2
    z_hi, z_lo = z // 2, z % 2
    units, width = out_ref.shape
    spans = chunks(units)
    count = len(spans)

    def device(z, x, y, c):
        return (z * wide + x, y * 2 + c)

    def along_x(s):
        return device(z, (x + s + wide) % wide, y, c)

    def along_z(r):
        return device((z + 2 * r + n_local) % n_local, x, y, c)

    z_pair = device(z_hi * 2 + 1 - z_lo, x, y, c)
    twin = device(z, x, y, 1 - c)

    def crossed(s, t):
        return device(
            z_hi * 2 + c, (x + s + wide) % wide, (y + t + halves) % halves, z_lo
        )

    moves = [(s, t) for t in range(halves) for s in range(wide)]
    stays = c == z_lo

    barrier = pltpu.get_barrier_semaphore()

    def greet(target):
        pl.semaphore_signal(
            barrier, inc=1, device_id=target, device_id_type=pl.DeviceIdType.MESH
        )

    greeted = [z_pair, twin, device(z_hi * 2 + 1 - z_lo, x, y, 1 - c)]
    for s in range(1, wide):
        greeted += [along_x(s), along_x(-s)]
    for r in range(1, halves):
        greeted += [along_z(r), along_z(-r)]
    for s, t in moves:
        if (s, t) != (0, 0):
            greeted += [crossed(s, t), crossed(-s, -t)]
    for target in greeted:
        greet(target)

    pl.semaphore_wait(barrier, len(greeted))

    def remote(source, target, sems, target_device):
        return pltpu.make_async_remote_copy(
            src_ref=source,
            dst_ref=target,
            send_sem=sems.at[0],
            recv_sem=sems.at[1],
            device_id=target_device,
            device_id_type=pl.DeviceIdType.MESH,
        )

    def span_of(k):
        return pl.ds(spans[k][0], spans[k][1] - spans[k][0])

    def slot(s, far):
        return hidden_ref if (s, far) == (0, 0) else whole.at[2 * s + far - 1]

    def z_copy(k):
        return remote(
            slot(0, 0).at[:, span_of(k)], slot(0, 1).at[:, span_of(k)], z_sem.at[k], z_pair
        )

    def x_copy(k, s, far):
        return remote(
            slot(0, far).at[:, span_of(k)],
            slot(s, far).at[:, span_of(k)],
            x_sem.at[k, s - 1, far],
            along_x(s),
        )

    def p_copy(k, r):
        return remote(
            going.at[r - 1, span_of(k)], coming.at[r - 1, span_of(k)],
            p_sem.at[k, r - 1], along_z(r),
        )

    def g_source(s):
        start = pl.multiple_of(((x + s) % wide) * width, 128)
        return grad_ref.at[:, pl.ds(start, width)]

    def g_copy(s, t):
        return remote(g_source(s), grads.at[t, z_lo, s], g_sem.at[t, s], crossed(s, t))

    def swap_copy(t):
        return remote(grads.at[t, c], grads.at[t, c], swap_sem.at[t], twin)

    def x_copies(k, far):
        return [x_copy(k, s, far) for s in range(1, wide)]

    def all_start(copies):
        for copy in copies:
            copy.start()

    def begin(k):
        z_copy(k).start()
        all_start(x_copies(k, 0))

    begin(0)
    own_copy = pltpu.make_async_copy(g_source(0), grads.at[0, z_lo, 0], own_sem)

    @pl.when(stays)
    def _():
        own_copy.start()

    @pl.when(jnp.logical_not(stays))
    def _():
        g_copy(0, 0).start()

    all_start([g_copy(s, t) for s, t in moves if (s, t) != (0, 0)])
    begin(1)
    z_copy(0).wait_recv()
    all_start(x_copies(0, 1))

    @pl.when(stays)
    def _():
        own_copy.wait()

    @pl.when(jnp.logical_not(stays))
    def _():
        g_copy(0, 0).wait()

    for t in range(halves):
        for s in range(wide):
            if (s, t) != (0, 0):
                g_copy(s, t).wait()
        swap_copy(t).start()
    for t in range(halves):
        swap_copy(t).wait()

    averaging = 1.0 / n_node

    def product(k, r, store):
        t = (y - z_hi - r + 2 * halves) % halves
        first, last = spans[k]

        @pl.loop(0, (last - first) // TILE)
        def _(i):
            at = pl.ds(pl.multiple_of(first + i * TILE, TILE), TILE)
            total = None
            for s in range(wide):
                for far in range(2):
                    b = z_lo if far == 0 else 1 - z_lo
                    part = lax.dot_general(
                        slot(s, far)[:, at], grads[t, b, s], (((0,), (0,)), ((), ())),
                        preferred_element_type=jnp.float32,
                    )
                    total = part if total is None else total + part
            store(at, total * averaging)

    def store_going(r):
        def store(at, value):
            going[r - 1, at, :] = value.astype(going.dtype)

        return store

    def store_out(at, value):
        out_ref[at, :] = value

    for k in range(count):
        if k + 2 < count:
            begin(k + 2)
        if k + 1 < count:
            z_copy(k + 1).wait_recv()
            all_start(x_copies(k + 1, 1))
        for copy in x_copies(k, 0) + x_copies(k, 1):
            copy.wait_recv()
        for r in range(1, halves):
            product(k, r, store_going(r))
            p_copy(k, r).start()
        product(k, 0, store_out)

    for k in range(count):
        for r in range(1, halves):
            p_copy(k, r).wait_recv()
        first, last = spans[k]

        @pl.loop(0, (last - first) // TILE)
        def _(i):
            at = pl.ds(pl.multiple_of(first + i * TILE, TILE), TILE)
            total = out_ref[at, :]
            for r in range(1, halves):
                total = total + coming[r - 1, at, :].astype(jnp.float32)
            out_ref[at, :] = total

    for k in range(count):
        z_copy(k).wait_send()
        for copy in x_copies(k, 0) + x_copies(k, 1):
            copy.wait_send()
        for r in range(1, halves):
            p_copy(k, r).wait_send()


def shards(gate_pre, up_pre, out_grad, n_node, n_local):
    wide, halves = n_node // n_local, n_local // 2
    gate_float = gate_pre.astype(jnp.float32)
    activated = gate_float * jax.nn.sigmoid(gate_float)
    hidden = (activated * up_pre.astype(jnp.float32)).astype(jnp.bfloat16)
    tokens, units = hidden.shape
    width = out_grad.shape[1] // wide
    count = len(WEIGHTS)
    return pl.pallas_call(
        functools.partial(kernel, n_node, n_local),
        out_shape=jax.ShapeDtypeStruct((units, width), jnp.float32),
        in_specs=[pl.BlockSpec(memory_space=pltpu.VMEM)] * 2,
        out_specs=pl.BlockSpec(memory_space=pltpu.VMEM),
        scratch_shapes=[
            pltpu.VMEM((2 * wide - 1, tokens, units), jnp.bfloat16),
            pltpu.VMEM((halves, 2, wide, tokens, width), jnp.bfloat16),
            pltpu.VMEM((halves - 1, units, width), jnp.bfloat16),
            pltpu.VMEM((halves - 1, units, width), jnp.bfloat16),
            pltpu.SemaphoreType.DMA((count, 2)),
            pltpu.SemaphoreType.DMA((count, wide - 1, 2, 2)),
            pltpu.SemaphoreType.DMA((count, halves - 1, 2)),
            pltpu.SemaphoreType.DMA((halves, wide, 2)),
            pltpu.SemaphoreType.DMA((halves, 2)),
            pltpu.SemaphoreType.DMA,
        ],
        compiler_params=pltpu.CompilerParams(
            collective_id=0, has_side_effects=True, vmem_limit_bytes=56 * 1024 * 1024
        ),
    )(hidden, out_grad)


def solution(mesh):
    placed = (P("node", "local"), P("node", "local"), P("node", "local"))
    return jax.shard_map(
        functools.partial(shards, n_node=mesh.shape["node"], n_local=mesh.shape["local"]),
        mesh=mesh,
        in_specs=placed,
        out_specs=P("local", "node"),
        check_vma=False,
    )
```

profile of v0, /device:TPU:0, one launch (start us, length us, event | category | flops | bytes accessed | tf_op | source)
XLA Modules:
  0.0 233.8 jit_solution(10181732872682154699)
XLA Ops:
  0.0 5.2 %fusion.4.hidden_ref = bf16[448,3840]{1,0:T(8,128)(2,1)} fusion(bf16[448,3840]{1,0:T(8,128)(2,1)} %param.4, bf16[448,3840]{1,0:T(8,128)(2,1)} %param.3), kind=kLoop, calls=%fused_computation.6 | loop fusion | flops 13762560 | bytes 10321920 | tf_op jit(solution)/shard_map/convert_element_type | solution.py:229
  5.2 221.2 %shard_map.37 = f32[3840,512]{1,0:T(8,128)} custom-call(bf16[448,3840]{1,0:T(8,128)(2,1)} %fusion.4.hidden_ref, bf16[448,1024]{1,0:T(8,128)(2,1)} %grad_ref.1), custom_call_target="tpu_custom_call" | custom-call | tf_op jit(solution)/shard_map/pallas_call | solution.py:233
  226.5 7.4 %copy.5 = f32[3840,512]{1,0:T(8,128)} copy(f32[3840,512]{1,0:T(8,128)} %shard_map.37) | data formatting | bytes 15728640
where the time goes:
time: 234 us
  Pallas kernels  221 us (94%)
  local copies, waits for them, and re-layouts  7.36 us (3%)
  other arithmetic  5.22 us (2%)
    pallas_call x1, Pallas kernels, shards(): pl.pallas_call(functools.partial(kernel, n_node, n_local), out_shape=jax....  221 us
    unnamed x1, local copies, waits for them, and re-layouts  7.36 us
    convert_element_type x1, other arithmetic, shards(): hidden = (activated * up_pre.astype(jnp.float32)).astype(jnp.bfloat16)  5.22 us

commit v1 on v0

v1 whole, which is shorter than its diff:
```python
import functools

import jax
import jax.numpy as jnp
from jax import lax
from jax.experimental import pallas as pl
from jax.experimental.pallas import tpu as pltpu
from jax.sharding import PartitionSpec as P

TILE = 128
LAG = 12
EARLY = 4
STRIPS = 2


def strips_of(width):
    return next(n for n in (STRIPS, 2, 1) if width % (n * TILE) == 0)


def kernel(
    n_node, n_local, gate_hbm, up_hbm, grad_hbm, out_ref,
    gate, up, own, hidden, grads, going, coming, giving,
    in_sem, own_sem, l_send, l_recv, g_sem, twin_sem, h_send, h_recv, p_sem, o_send, o_recv,
):
    wide, deep, tall = n_node // n_local, n_local, n_local // 2
    layers = deep // 2
    node, local = lax.axis_index("node"), lax.axis_index("local")
    z, x, y, c = node // wide, node % wide, local // 2, local % 2
    side = z // layers
    tokens, units = gate.shape
    width = out_ref.shape[1]
    count = units // TILE
    strips = strips_of(width)
    strip = width // strips
    slots = layers * wide
    averaging = 1.0 / n_node

    def depth(zz):
        return jnp.where(zz < layers, layers - 1 - zz, zz - layers)

    def layer(half, d):
        return jnp.where(half == 0, layers - 1 - d, layers + d)

    mine = depth(z)
    inside = mine == 0
    outside = jnp.logical_not(inside)
    inner_z = layer(side, 0)
    mirror = (layer(1 - side, 0) * wide + x, local)
    twin = (node, y * 2 + 1 - c)

    def device(zz, xx, yy, cc):
        return (zz * wide + xx, yy * 2 + cc)

    def beside(i):
        return (x + i) % wide

    def slot_of(d, xx):
        return d * wide + xx

    my_slot = slot_of(mine, x)

    def rows(slot):
        return pl.ds(pl.multiple_of(slot * tokens, 16), tokens)

    def chunk(k):
        return pl.ds(pl.multiple_of(k * TILE, TILE), TILE)

    def remote(source, target, send, recv, where):
        return pltpu.make_async_remote_copy(
            src_ref=source, dst_ref=target, send_sem=send, recv_sem=recv,
            device_id=where, device_id_type=pl.DeviceIdType.MESH,
        )

    def loads(k):
        return [
            pltpu.make_async_copy(gate_hbm.at[:, chunk(k)], gate.at[:, chunk(k)], in_sem.at[k, 0]),
            pltpu.make_async_copy(up_hbm.at[:, chunk(k)], up.at[:, chunk(k)], in_sem.at[k, 1]),
        ]

    own_load = pltpu.make_async_copy(grad_hbm, own, own_sem)
    own_load.start()
    for copy in loads(0):
        copy.start()

    @pl.loop(1, count)
    def _(k):
        for copy in loads(k):
            copy.start()

    barrier = pltpu.get_barrier_semaphore()

    def greet(target):
        pl.semaphore_signal(
            barrier, inc=1, device_id=target, device_id_type=pl.DeviceIdType.MESH
        )

    ring = [(i, j, m) for i in range(wide) for j in range(tall) for m in range(2)]

    @pl.when(inside)
    def _():
        greet(mirror)
        for d in range(layers):
            for i, j, m in ring:
                if (d, i, j, m) != (0, 0, 0, 0):
                    greet(device(layer(side, d), beside(i), (y + j) % tall, (c + m) % 2))
        pl.semaphore_wait(barrier, layers * len(ring))

    layer_mates = [(i, j) for i in range(wide) for j in range(tall) if (i, j) != (0, 0)]

    @pl.when(outside)
    def _():
        for i, j, m in ring:
            greet(device(inner_z, beside(i), (y + j) % tall, (c + m) % 2))
        for i, j in layer_mates:
            greet(device(z, beside(i), (y + j) % tall, c))
        pl.semaphore_wait(barrier, len(ring) + len(layer_mates))

    half = tall // 2

    def row_of(near, i):
        low, high = i, tall - 1 - i
        return jnp.where((side == 0) == near, low, high)

    def entry(near, i, cc):
        return (layers if near else 0) + depth(row_of(near, i) * 2 + cc)

    own_near = jnp.where(y >= half, 1, 0) == side
    own_low = y < half
    own_at = jnp.where(own_near, half, 0) + jnp.where(own_low, y, tall - 1 - y)
    own_entry = jnp.where(own_near, layers, 0) + depth(y * 2 + c)

    def share_source(t, i, held):
        return held.at[:, pl.ds(pl.multiple_of(beside(i) * width + t * strip, TILE), strip)]

    def share_target(t):
        return grads.at[own_entry, rows(my_slot), pl.ds(t * strip, strip)]

    def share(t, i, j):
        return remote(
            share_source(t, i, own), share_target(t), l_send.at[t, i * tall + j], l_recv.at[own_at, t, x],
            device(z, beside(i), (y + j) % tall, c),
        )

    def keep(t):
        return pltpu.make_async_copy(share_source(t, 0, grad_hbm), share_target(t), l_recv.at[own_at, t, x])

    own_load.wait()
    for t in range(strips):
        for i, j in layer_mates:
            share(t, i, j).start()
    for t in range(strips):
        keep(t).start()

    def layer_rows(d):
        return pl.ds(pl.multiple_of(d * (wide * tokens), 16), wide * tokens)

    def shared(near, i, t):
        for xx in range(wide):
            part = grads.at[entry(near, i, c), rows(slot_of(mine, xx)), pl.ds(t * strip, strip)]
            pltpu.make_async_copy(part, part, l_recv.at[near * half + i, t, xx]).wait()

    def g_copy(near, i, t, d):
        part = grads.at[entry(near, i, c), layer_rows(d), pl.ds(t * strip, strip)]
        at = near * half + i
        return remote(
            part, part, g_sem.at[at, t, d - 1, 0], g_sem.at[at, t, d - 1, 1],
            device(inner_z, x, y, c),
        )

    def each_depth(act):
        for d in range(1, layers):
            @pl.when(mine == d)
            def _():
                act(d)

    def g_start(near, t):
        for i in range(half):
            shared(near, i, t)
            each_depth(lambda d: g_copy(near, i, t, d).start())

    def twin_copy(near, i, t, cc):
        part = grads.at[entry(near, i, cc), :, pl.ds(t * strip, strip)]
        at = near * half + i
        return remote(part, part, twin_sem.at[at, t, 0], twin_sem.at[at, t, 1], twin)

    def g_pass(near, t):
        for i in range(half):
            shared(near, i, t)
            for d in range(1, layers):
                g_copy(near, i, t, d).wait_recv()
            twin_copy(near, i, t, c).start()

    def g_passed(near, t):
        for i in range(half):
            twin_copy(near, i, t, 1 - c).wait_recv()

    step = next(b for b in (128, 112, 96, 64, 32, 16) if tokens % b == 0)

    def activate(k):
        for copy in loads(k):
            copy.wait()
        at = chunk(k)
        for first in range(0, tokens, step):
            g = gate[pl.ds(first, step), at].astype(jnp.float32)
            u = up[pl.ds(first, step), at].astype(jnp.float32)
            value = g * jax.nn.sigmoid(g) * u
            into = pl.ds(pl.multiple_of(my_slot * tokens + first, 16), step)
            hidden[into, at] = value.astype(hidden.dtype)

    def h_copy(k, slot, index, where):
        part = hidden.at[rows(slot), chunk(k)]
        return remote(part, part, h_send.at[k, index], h_recv.at[k, slot], where)

    def here(k, i):
        return h_copy(k, my_slot, i, device(z, beside(i), y, c))

    def inward(k):
        return h_copy(k, my_slot, 0, device(inner_z, x, y, c))

    def relay_out(k, i):
        return h_copy(k, slot_of(mine, beside(i)), wide + i - 1, device(inner_z, x, y, c))

    def relay_in(k, d, i):
        return h_copy(k, slot_of(d, x), d * wide + i, device(z, beside(i), y, c))

    def early(k):
        return k % 3 == 2

    def late(k):
        return k % 3 != 2

    def send_in(k):
        activate(k)
        for i in range(1, wide):
            here(k, i).start()

    def send_out(k):
        activate(k)
        inward(k).start()

        @pl.when(early(k))
        def _():
            for i in range(1, wide):
                here(k, i).start()

    def pass_out(k):
        @pl.when(early(k))
        def _():
            for i in range(1, wide):
                h_copy(k, slot_of(mine, beside(i)), 0, twin).wait_recv()
                relay_out(k, i).start()

    def pass_in(k):
        for d in range(1, layers):
            h_copy(k, slot_of(d, x), 0, twin).wait_recv()

            @pl.when(late(k))
            def _():
                for i in range(1, wide):
                    relay_in(k, d, i).start()

    def gathered(k):
        for d in range(layers):
            for i in range(1, wide):
                h_copy(k, slot_of(d, beside(i)), 0, twin).wait_recv()

    def product(k, index, at):
        return lax.dot_general(
            hidden[:, chunk(k)], grads[index, :, at], (((0,), (0,)), ((), ())),
            preferred_element_type=jnp.float32,
        ) * averaging

    def p_copy(k, index, at):
        return remote(
            going.at[index, chunk(k), at], coming.at[index, chunk(k), at],
            p_sem.at[k, index, 0], p_sem.at[k, index, 1], mirror,
        )

    whole = pl.ds(0, width)

    def far(k, i, cc, at):
        index = entry(False, i, cc)
        going[index, chunk(k), at] = product(k, index, at).astype(going.dtype)
        p_copy(k, index, at).start()

    def o_copy(k, d):
        return remote(
            giving.at[d - 1, chunk(k)], out_ref.at[chunk(k)],
            o_send.at[k, d - 1], o_recv.at[k], device(layer(side, d), x, y, c),
        )

    def near(k):
        for d in reversed(range(layers)):
            p_copy(k, d, whole).wait_recv()
            total = product(k, layers + d, whole) + coming[d, chunk(k)].astype(jnp.float32)
            if d:
                giving[d - 1, chunk(k)] = total.astype(giving.dtype)
                o_copy(k, d).start()
            else:
                out_ref[chunk(k)] = total.astype(out_ref.dtype)

    first_c = 1 - side

    @pl.when(inside)
    def _():
        send_in(0)
        send_in(1)
        pass_in(0)
        g_pass(False, 0)
        for t in range(strips):
            if t:
                g_pass(False, t)
            for k in range(EARLY):
                if t == 0:
                    send_in(k + 2)
                    pass_in(k + 1)
                    gathered(k)
                for i in range(half):
                    far(k, i, c, pl.ds(t * strip, strip))
                if k == 0:
                    g_passed(False, t)
                for i in range(half):
                    far(k, i, 1 - c, pl.ds(t * strip, strip))

        def body(k):
            @pl.when(k + 2 < count)
            def _():
                send_in(k + 2)

            @pl.when(k + 1 < count)
            def _():
                pass_in(k + 1)

            gathered(k)
            for i in range(half):
                far(k, i, first_c, whole)
                far(k, i, 1 - first_c, whole)

        @pl.loop(EARLY, LAG)
        def _(k):
            body(k)

        for t in range(strips):
            g_pass(True, t)
        for t in range(strips):
            g_passed(True, t)

        @pl.loop(LAG, count)
        def _(k):
            body(k)
            near(k - LAG)

        @pl.loop(count - LAG, count)
        def _(k):
            near(k)

        @pl.loop(0, count)
        def _(k):
            for i in range(1, wide):
                here(k, i).wait_send()

            @pl.when(late(k))
            def _():
                for d in range(1, layers):
                    for i in range(1, wide):
                        relay_in(k, d, i).wait_send()

            for d in range(layers):
                p_copy(k, d, whole).wait_send()
            for d in range(1, layers):
                o_copy(k, d).wait_send()

        for near_too in (False, True):
            for t in range(strips):
                for i in range(half):
                    twin_copy(near_too, i, t, c).wait_send()

    @pl.when(outside)
    def _():
        send_out(0)
        g_start(False, 0)
        send_out(1)
        pass_out(0)
        for t in range(1, strips):
            g_start(False, t)

        @pl.loop(2, count)
        def _(k):
            for t in range(strips):
                @pl.when(k == EARLY + 2 + 2 * t)
                def _():
                    g_start(True, t)

            send_out(k)
            pass_out(k - 1)

        pass_out(count - 1)

        @pl.loop(0, count)
        def _(k):
            inward(k).wait_send()

            @pl.when(early(k))
            def _():
                for i in range(1, wide):
                    here(k, i).wait_send()
                    relay_out(k, i).wait_send()

            pltpu.make_async_copy(
                out_ref.at[chunk(k)], out_ref.at[chunk(k)], o_recv.at[k]
            ).wait()

        for near_too in (False, True):
            for t in range(strips):
                for i in range(half):
                    each_depth(lambda d: g_copy(near_too, i, t, d).wait_send())

    for t in range(strips):
        for i, j in layer_mates:
            share(t, i, j).wait_send()


def shards(gate_pre, up_pre, out_grad, n_node, n_local):
    wide, layers, tall = n_node // n_local, n_local // 2, n_local // 2
    tokens, units = gate_pre.shape
    width = out_grad.shape[1] // wide
    count = units // TILE
    strips = strips_of(width)
    slots = layers * wide
    half = gate_pre.dtype
    dma = pltpu.SemaphoreType.DMA
    result = pl.pallas_call(
        functools.partial(kernel, n_node, n_local),
        out_shape=OUT((units, width), half),
        in_specs=[pl.BlockSpec(memory_space=pl.ANY)] * 3,
        out_specs=pl.BlockSpec(memory_space=pltpu.VMEM),
        scratch_shapes=[
            pltpu.VMEM((tokens, units), half),
            pltpu.VMEM((tokens, units), half),
            pltpu.VMEM((tokens, wide * width), half),
            pltpu.VMEM((slots * tokens, units), half),
            pltpu.VMEM((2 * layers, slots * tokens, width), half),
            pltpu.VMEM((layers, units, width), half),
            pltpu.VMEM((layers, units, width), half),
            pltpu.VMEM((layers - 1, units, width), half),
            dma((count, 2)),
            dma,
            dma((strips, wide * tall)),
            dma((tall, strips, wide)),
            dma((tall, strips, layers - 1, 2)),
            dma((tall, strips, 2)),
            dma((count, slots)),
            dma((count, slots)),
            dma((count, layers, 2)),
            dma((count, layers - 1)),
            dma((count,)),
        ],
        compiler_params=pltpu.CompilerParams(
            collective_id=0, has_side_effects=True, vmem_limit_bytes=62 * 1024 * 1024
        ),
    )(gate_pre, up_pre, out_grad)
    return result.astype(jnp.float32)


OUT = jax.ShapeDtypeStruct


def solution(mesh):
    placed = (P("node", "local"), P("node", "local"), P("node", "local"))
    return jax.shard_map(
        functools.partial(shards, n_node=mesh.shape["node"], n_local=mesh.shape["local"]),
        mesh=mesh,
        in_specs=placed,
        out_specs=P("local", "node"),
        check_vma=False,
    )
```

time: 234 us -> 229 us (0.979); the launches traced: 234 us -> 226 us
  local copies, waits for them, and re-layouts: 7.36 us -> 0 us
    unnamed x1 -> x0, local copies, waits for them, and re-layouts: 7.36 us -> none
where the time goes in v1:
time: 229 us; the launch traced here: 226 us
  Pallas kernels  220 us (96%)
  other arithmetic  6.46 us (3%)
    pallas_call x1, Pallas kernels, shards(): pl.pallas_call(functools.partial(kernel, n_node, n_local), out_shape=OUT(...  220 us
    convert_element_type x1, other arithmetic, shards(): return result.astype(jnp.float32)  6.46 us

profile of v1, /device:TPU:0, one launch (start us, length us, event | category | flops | bytes accessed | tf_op | source)
XLA Modules:
  0.0 226.2 jit_solution(17289761143494889006)
XLA Ops:
  0.0 219.8 %shard_map.37 = bf16[3840,512]{1,0:T(8,128)(2,1)} custom-call(bf16[448,3840]{1,0:T(8,128)(2,1)} %gate_hbm.1, bf16[448,3840]{1,0:T(8,128)(2,1)} %up_hbm.1, bf16[448,1024]{1,0:T(8,128)(2,1)} %grad_hbm.1), custom_call_target="tpu_custom_call" | custom-call | tf_op jit(solution)/shard_map/pallas_call | solution.py:432
  219.8 6.5 %convert_element_type.3 = f32[3840,512]{1,0:T(8,128)} convert(bf16[3840,512]{1,0:T(8,128)(2,1)} %shard_map.37) | non-fusion elementwise | flops 1966080 | bytes 11796480 | tf_op jit(solution)/shard_map/convert_element_type | solution.py:462

commit v2 on v1

--- a/solution.py
+++ b/solution.py
@@ -10,7 +10,9 @@
 TILE = 128
 LAG = 12
 EARLY = 4
-STRIPS = 2
+RAMP = 0
+DEPTH = 2
+STRIPS = 4
 
 
 def strips_of(width):
@@ -250,6 +252,15 @@
                 h_copy(k, slot_of(mine, beside(i)), 0, twin).wait_recv()
                 relay_out(k, i).start()
 
+    def drain(k):
+        inward(k).wait_send()
+
+        @pl.when(early(k))
+        def _():
+            for i in range(1, wide):
+                here(k, i).wait_send()
+                relay_out(k, i).wait_send()
+
     def pass_in(k):
         for d in range(1, layers):
             h_copy(k, slot_of(d, x), 0, twin).wait_recv()
@@ -277,6 +288,9 @@
         )
 
     whole = pl.ds(0, width)
+
+    def lane(t):
+        return pl.ds(t * strip, strip)
 
     def far(k, i, cc, at):
         index = entry(False, i, cc)
@@ -306,37 +320,50 @@
         send_in(0)
         send_in(1)
         pass_in(0)
-        g_pass(False, 0)
-        for t in range(strips):
-            if t:
-                g_pass(False, t)
-            for k in range(EARLY):
-                if t == 0:
-                    send_in(k + 2)
-                    pass_in(k + 1)
-                    gathered(k)
+        for n in range(EARLY):
+            send_in(n + 2)
+            if n < strips:
+                g_pass(False, n)
+            pass_in(n + 1)
+            gathered(n)
+            for t in range(min(n, strips)):
                 for i in range(half):
-                    far(k, i, c, pl.ds(t * strip, strip))
-                if k == 0:
-                    g_passed(False, t)
-                for i in range(half):
-                    far(k, i, 1 - c, pl.ds(t * strip, strip))
-
-        def body(k):
-            @pl.when(k + 2 < count)
-            def _():
-                send_in(k + 2)
-
-            @pl.when(k + 1 < count)
-            def _():
-                pass_in(k + 1)
-
+                    far(n, i, c, lane(t))
+                    far(n, i, 1 - c, lane(t))
+            if n < strips:
+                for k in range(n + 1):
+                    for i in range(half):
+                        far(k, i, c, lane(n))
+                g_passed(False, n)
+                for k in range(n + 1):
+                    for i in range(half):
+                        far(k, i, 1 - c, lane(n))
+
+        def multiply(k):
             gathered(k)
             for i in range(half):
                 far(k, i, first_c, whole)
                 far(k, i, 1 - first_c, whole)
 
-        @pl.loop(EARLY, LAG)
+        @pl.loop(EARLY, EARLY + RAMP)
+        def _(k):
+            for m in range(2):
+                send_in(2 * k - EARLY + 2 + m)
+                pass_in(2 * k - EARLY + 1 + m)
+            multiply(k)
+
+        def body(k):
+            @pl.when(k + RAMP + 2 < count)
+            def _():
+                send_in(k + RAMP + 2)
+
+            @pl.when(k + RAMP + 1 < count)
+            def _():
+                pass_in(k + RAMP + 1)
+
+            multiply(k)
+
+        @pl.loop(EARLY + RAMP, LAG)
         def _(k):
             body(k)
 
@@ -378,34 +405,33 @@
     @pl.when(outside)
     def _():
         send_out(0)
-        g_start(False, 0)
-        send_out(1)
-        pass_out(0)
-        for t in range(1, strips):
-            g_start(False, t)
-
-        @pl.loop(2, count)
+        for n in range(EARLY):
+            if n < strips:
+                g_start(False, n)
+            if n + 1 >= DEPTH:
+                drain(n + 1 - DEPTH)
+            send_out(n + 1)
+            pass_out(n)
+
+        @pl.loop(EARLY + 1, count)
         def _(k):
             for t in range(strips):
-                @pl.when(k == EARLY + 2 + 2 * t)
+                @pl.when(k == EARLY + 1 + t)
                 def _():
                     g_start(True, t)
 
+            drain(k - DEPTH)
             send_out(k)
             pass_out(k - 1)
 
         pass_out(count - 1)
 
+        @pl.loop(count - DEPTH, count)
+        def _(k):
+            drain(k)
+
         @pl.loop(0, count)
         def _(k):
-            inward(k).wait_send()
-
-            @pl.when(early(k))
-            def _():
-                for i in range(1, wide):
-                    here(k, i).wait_send()
-                    relay_out(k, i).wait_send()
-
             pltpu.make_async_copy(
                 out_ref.at[chunk(k)], out_ref.at[chunk(k)], o_recv.at[k]
             ).wait()
@@ -456,13 +482,13 @@
             dma((count,)),
         ],
         compiler_params=pltpu.CompilerParams(
-            collective_id=0, has_side_effects=True, vmem_limit_bytes=62 * 1024 * 1024
+            collective_id=0, has_side_effects=True, vmem_limit_bytes=56 * 1024 * 1024
         ),
     )(gate_pre, up_pre, out_grad)
     return result.astype(jnp.float32)
 
 
-OUT = jax.ShapeDtypeStruct
+OUT = pltpu.VMEM
 
 
 def solution(mesh):

time: 229 us -> 221 us (0.965); the launches traced: 226 us -> 221 us
  Pallas kernels: 220 us -> 217 us
    pallas_call x1, Pallas kernels: 220 us -> 217 us  [shards(): pl.pallas_call(functools.partial(kernel, n_node, n_local), out_shape=OUT(...]
where the time goes in v2:
time: 221 us
  Pallas kernels  217 us (98%)
  other arithmetic  4.35 us (2%)
    pallas_call x1, Pallas kernels, shards(): pl.pallas_call(functools.partial(kernel, n_node, n_local), out_shape=OUT(...  217 us

profile of v2, /device:TPU:0, one launch (start us, length us, event | category | flops | bytes accessed | tf_op | source)
XLA Modules:
  0.0 221.1 jit_solution(17859806084147125909)
XLA Ops:
  0.0 216.8 %shard_map.37 = bf16[3840,512]{1,0:T(8,128)(2,1)S(1)} custom-call(bf16[448,3840]{1,0:T(8,128)(2,1)} %gate_hbm.1, bf16[448,3840]{1,0:T(8,128)(2,1)} %up_hbm.1, bf16[448,1024]{1,0:T(8,128)(2,1)} %grad_hbm.1), custom_call_target="tpu_custom_call" | custom-call | tf_op jit(solution)/shard_map/pallas_call | solution.py:458
  216.8 4.3 %convert_element_type.3 = f32[3840,512]{1,0:T(8,128)} convert(bf16[3840,512]{1,0:T(8,128)(2,1)S(1)} %shard_map.37) | non-fusion elementwise | flops 1966080 | bytes 11796480 | tf_op jit(solution)/shard_map/convert_element_type | solution.py:488
